TPU v7x, 32 devices: a whole 2x2x4 slice. The times are simulated.
32 devices in a mesh: seq: 8 (over z, y), batch: 4 (over x, core).
Axes of the slice: x: 2, y: 2, z: 4, core: 2. Of those that a mesh axis runs over, the one named last changes fastest.
Arguments:
- inputs: bfloat16 [8192, 4096], P(('batch', 'seq')), parts along dimension 0, may hold values from -6 to 6
- recur_weight: bfloat16 [16, 256, 256], replicated, may hold values from -0.375 to 0.375
- input_weight: bfloat16 [16, 256, 256], replicated, may hold values from -0.375 to 0.375
- recur_bias: float32 [4096], replicated, may hold values from -4 to 4
- input_bias: float32 [4096], replicated, may hold values from -4 to 4
- decay_rate: float32 [4096], replicated, may hold values from 4.8828124e-06 to 0.02
- kv_weight: bfloat16 [4096, 512], replicated, may hold values from -61 to 61
Outputs:
- attended: bfloat16 [8192, 4096], P(('batch', 'seq')), parts along dimension 0
There are 4 independent parts, one for each index of `batch`. A program takes and returns all parts, laid end to end along the dimension named above; an argument that names none is the same for every part. Nothing has to cross between parts.
All inputs are finite; a program needn't handle non-finite values.
Results may differ from a plain program's by a relative error of at most 0.03.
Values may be sent and summed in bfloat16 or wider, within the bound.
A program may use at most 128 MiB of HBM per device.

v0:
```python
import functools
import math

import jax
import jax.numpy as jnp
from jax import lax
from jax.experimental import pallas as pl
from jax.experimental.pallas import tpu as pltpu
from jax.sharding import PartitionSpec as P

WINDOW = 2048
SUB = 8
PIECES = 2
MESH = pl.DeviceIdType.MESH
LOG2E = math.log2(math.e)
F32 = jnp.float32
BF16 = jnp.bfloat16


def dot(a, b):
    return jnp.dot(a, b, preferred_element_type=F32)


def dot_t(a, b):
    return lax.dot_general(a, b, (((1,), (1,)), ((), ())), preferred_element_type=F32)


def fused(
    n, cols, reach, scale,
    x_hbm, rw_hbm, iw_hbm, rb, ib, dr, kvw_hbm,
    out,
    xv, rwv, iwv, kvw, perm, unperm, pre_a, pre_b, cum, loc, seg_a, seg_s, sum_send, sum_recv,
    carry, hid, qn, kvb, top, low, acc, bias,
    in_sem, kvw_sem, s_send, s_recv, z_send, y_send, kv_recv,
):
    me = lax.axis_index("seq")
    row = me // cols
    col = me % cols
    blocks, tok, width = xv.shape
    seg = tok // SUB
    groups = blocks // 2
    head_dim = width
    levels = z_send.shape[0] - 1
    piece_rows = tok // PIECES

    def in_copies(b):
        at = pl.ds(pl.multiple_of(b * width, width), width)
        return (
            pltpu.make_async_copy(x_hbm.at[:, at], xv.at[b], in_sem.at[0, b]),
            pltpu.make_async_copy(rw_hbm.at[b], rwv.at[b], in_sem.at[1, b]),
            pltpu.make_async_copy(iw_hbm.at[b], iwv.at[b], in_sem.at[2, b]),
        )

    @pl.loop(0, blocks)
    def _(b):
        for copy in in_copies(b):
            copy.start()

    kvw_copy = pltpu.make_async_copy(kvw_hbm, kvw, kvw_sem)
    kvw_copy.start()

    barrier = pltpu.get_barrier_semaphore()

    @pl.loop(1, n)
    def _(d):
        pl.semaphore_signal(
            barrier, inc=1, device_id={"seq": lax.rem(me + d, n)}, device_id_type=MESH
        )

    first = lax.broadcasted_iota(jnp.int32, (tok, tok), 0)
    second = lax.broadcasted_iota(jnp.int32, (tok, tok), 1)
    place_1 = second // SUB + seg * (second % SUB)
    place_0 = first // SUB + seg * (first % SUB)
    perm[...] = jnp.where(second == place_0, 1.0, 0.0).astype(BF16)
    unperm[...] = jnp.where(first == place_1, 1.0, 0.0).astype(BF16)
    bias[...] = jnp.where(place_1 <= first, 0.0, -1e30)

    def mats(b, pre):
        for copy in in_copies(b):
            copy.wait()
        moved = dot(perm[...], xv[b])
        small = moved.astype(BF16)
        pre[0] = moved
        pre[1] = dot(small, rwv[b])
        pre[2] = dot(small, iwv[b])

    def gates(b, g, half, pre):
        at = pl.ds(pl.multiple_of(b * width, width), width)
        rbias = jnp.broadcast_to(rb[:, at], (SUB, width))
        ibias = jnp.broadcast_to(ib[:, at], (SUB, width))
        rate = jnp.broadcast_to(dr[:, at] * (-8.0 * LOG2E), (SUB, width))
        prod = None
        state = None
        for k in range(seg):
            rows = slice(k * SUB, (k + 1) * SUB)
            rec = 0.5 * jnp.tanh(0.5 * (pre[1, rows, :] + rbias)) + 0.5
            gate = 0.5 * jnp.tanh(0.5 * (pre[2, rows, :] + ibias)) + 0.5
            step = jnp.exp2(rec * rate)
            drive = jnp.sqrt(1.0 - step * step) * (gate * pre[0, rows, :])
            prod = step if k == 0 else prod * step
            state = drive if k == 0 else step * state + drive
            cum[b, rows, :] = prod
            loc[b, rows, :] = state
        cs = jnp.zeros((1, width), F32)
        cp = jnp.ones((1, width), F32)
        for j in range(SUB):
            seg_s[b, j : j + 1, :] = cs
            seg_a[b, j : j + 1, :] = cp
            cs = prod[j : j + 1] * cs + state[j : j + 1]
            cp = prod[j : j + 1] * cp
        lanes = slice(half * width, (half + 1) * width)
        sum_send[g, 0:1, lanes] = cp
        sum_send[g, 1:2, lanes] = cs

    def send_summary(g):
        @pl.loop(me + 1, n)
        def _(to):
            pltpu.make_async_remote_copy(
                src_ref=sum_send.at[g],
                dst_ref=sum_recv.at[me, g],
                send_sem=s_send.at[to],
                recv_sem=s_recv.at[me],
                device_id={"seq": to},
                device_id_type=MESH,
            ).start()

    def summary_slab(other):
        return pltpu.make_async_remote_copy(
            src_ref=sum_send,
            dst_ref=sum_recv.at[other],
            send_sem=s_send.at[other],
            recv_sem=s_recv.at[other],
            device_id={"seq": other},
            device_id_type=MESH,
        )

    mats(0, pre_a)
    pl.semaphore_wait(barrier, n - 1)

    @pl.loop(0, groups - 1)
    def _(g):
        mats(2 * g + 1, pre_b)
        gates(2 * g, g, 0, pre_a)
        mats(2 * g + 2, pre_a)
        gates(2 * g + 1, g, 1, pre_b)
        send_summary(g)

    mats(blocks - 1, pre_b)
    gates(blocks - 2, groups - 1, 0, pre_a)
    gates(blocks - 1, groups - 1, 1, pre_b)
    send_summary(groups - 1)

    def fold(other, state):
        summary_slab(other).wait_recv()
        return tuple(
            sum_recv[other, g, 0:1, :] * state[g] + sum_recv[other, g, 1:2, :]
            for g in range(groups)
        )

    entering = lax.fori_loop(
        0, me, fold, tuple(jnp.zeros((1, 2 * width), F32) for _ in range(groups))
    )
    for g in range(groups):
        carry[2 * g] = entering[g][:, :width]
        carry[2 * g + 1] = entering[g][:, width:]

    @pl.loop(0, blocks)
    def _(b):
        at = pl.ds(pl.multiple_of(b * width, width), width)
        into = seg_s[b] + seg_a[b] * carry[b]
        for k in range(seg // 2):
            rows = slice(2 * k * SUB, (2 * k + 2) * SUB)
            twice = jnp.concatenate([into, into], axis=0)
            hid[rows, at] = (loc[b, rows, :] + cum[b, rows, :] * twice).astype(BF16)

    kvw_copy.wait()
    kvb[me] = dot(hid[...], kvw[...]).astype(BF16)

    def z_copy(s, m, piece):
        rows = pl.ds(piece * piece_rows, piece_rows)
        return pltpu.make_async_remote_copy(
            src_ref=kvb.at[s, rows],
            dst_ref=kvb.at[s, rows],
            send_sem=z_send.at[m, piece],
            recv_sem=kv_recv.at[s, piece],
            device_id={"seq": me + cols},
            device_id_type=MESH,
        )

    def y_copy(s, m, piece, delta):
        rows = pl.ds(piece * piece_rows, piece_rows)
        to = row * cols + lax.rem(col + delta, cols)
        return pltpu.make_async_remote_copy(
            src_ref=kvb.at[s, rows],
            dst_ref=kvb.at[s, rows],
            send_sem=y_send.at[delta - 1, m, piece],
            recv_sem=kv_recv.at[s, piece],
            device_id={"seq": to},
            device_id_type=MESH,
        )

    def arrived(s, piece):
        rows = pl.ds(piece * piece_rows, piece_rows)
        pltpu.make_async_remote_copy(
            src_ref=kvb.at[s, rows],
            dst_ref=kvb.at[s, rows],
            send_sem=z_send.at[0, piece],
            recv_sem=kv_recv.at[s, piece],
            device_id={"seq": lax.rem(me + cols, n)},
            device_id_type=MESH,
        ).wait_recv()

    def goes_up(m):
        return (me + cols < n) & (cols * (m + 1) <= reach + cols - 1)

    def goes_over(s, delta):
        far = row * cols + lax.rem(col + delta, cols) - s
        return (far >= 1) & (far <= reach)

    def forward(s, m, piece):
        @pl.when(goes_up(m))
        def _():
            z_copy(s, m, piece).start()

        for delta in range(1, cols):
            @pl.when(goes_over(s, delta))
            def _():
                y_copy(s, m, piece, delta).start()

    for piece in range(PIECES):
        forward(me, 0, piece)

    factor = scale * LOG2E

    @pl.loop(0, blocks, step=2)
    def _(base):
        for h in (base, base + 1):
            at = pl.ds(pl.multiple_of(h * width, width), width)
            query = dot(unperm[...], hid[:, at]).astype(BF16)
            qn[h] = query
            scores = dot_t(query, kvb[me, :, :head_dim]) + bias[...]
            highest = jnp.max(scores, axis=1, keepdims=True)
            expo = jnp.exp2((scores - highest) * factor)
            top[h] = jnp.broadcast_to(highest, (tok, 128))
            low[h] = functools.reduce(
                jnp.add, [expo[:, c : c + 128] for c in range(0, tok, 128)]
            )
            acc[h] = dot(expo.astype(BF16), kvb[me, :, head_dim:])

    def attend(s, far, masked):
        @pl.loop(0, blocks, step=2)
        def _(base):
            for h in (base, base + 1):
                scores = dot_t(qn[h], kvb[s, :, :head_dim])
                if masked:
                    qrow = lax.broadcasted_iota(jnp.int32, (tok, tok), 0)
                    krow = lax.broadcasted_iota(jnp.int32, (tok, tok), 1)
                    krow = krow // SUB + seg * (krow % SUB)
                    scores = jnp.where(far * tok + qrow - krow < WINDOW, scores, -1e30)
                before = top[h]
                highest = jnp.maximum(before, jnp.max(scores, axis=1, keepdims=True))
                shrink = jnp.exp2((before - highest) * factor)
                parts = [
                    jnp.exp2((scores[:, c : c + 128] - highest) * factor)
                    for c in range(0, tok, 128)
                ]
                top[h] = highest
                low[h] = low[h] * shrink + functools.reduce(jnp.add, parts)
                expo = jnp.concatenate([p.astype(BF16) for p in parts], axis=1)
                update = dot(expo, kvb[s, :, head_dim:])
                for c in range(0, head_dim, 128):
                    acc[h, :, c : c + 128] = (
                        acc[h, :, c : c + 128] * shrink + update[:, c : c + 128]
                    )

    partial = reach * tok + tok - 1 >= WINDOW

    @pl.loop(1, levels + 2)
    def _(m):
        mine = me - cols * m
        held = (m <= levels) & (mine >= 0) & (cols * m <= reach + cols - 1)

        @pl.when(held)
        def _():
            for piece in range(PIECES):
                arrived(mine, piece)
                forward(mine, m, piece)

        @pl.loop(1, cols + 1)
        def _(delta):
            own = delta // cols
            s = row * cols + lax.rem(col + delta, cols) - cols * (m - 1 + own)
            far = me - s
            wanted = (s >= 0) & (far >= 1) & (far <= reach)
            wanted = wanted & (m - 1 + own <= levels)

            @pl.when(wanted & (own == 0))
            def _():
                for piece in range(PIECES):
                    arrived(s, piece)

            if partial:
                @pl.when(wanted & (far * tok + tok - 1 < WINDOW))
                def _():
                    attend(s, far, False)

                @pl.when(wanted & (far * tok + tok - 1 >= WINDOW))
                def _():
                    attend(s, far, True)
            else:
                @pl.when(wanted)
                def _():
                    attend(s, far, False)

    @pl.loop(0, blocks)
    def _(h):
        at = pl.ds(pl.multiple_of(h * width, width), width)
        total = jnp.sum(low[h], axis=1, keepdims=True)
        out[:, at] = (acc[h] * (1.0 / total)).astype(BF16)

    @pl.loop(me + 1, n)
    def _(to):
        summary_slab(to).wait_send()

    @pl.loop(0, levels + 1)
    def _(m):
        s = me - cols * m
        held = (s >= 0) & (cols * m <= reach + cols - 1)
        for piece in range(PIECES):
            @pl.when(held & goes_up(m))
            def _():
                z_copy(s, m, piece).wait_send()

            for delta in range(1, cols):
                @pl.when(held & goes_over(s, delta))
                def _():
                    y_copy(s, m, piece, delta).wait_send()


def on_device(n, inputs, recur_weight, input_weight, recur_bias, input_bias, decay_rate, kv_weight):
    tok, full = inputs.shape
    blocks, width = recur_weight.shape[:2]
    cols = 1
    while 4 * cols * cols <= n:
        cols *= 2
    reach = min((WINDOW + tok - 2) // tok, n - 1)
    levels = min((reach + cols - 1) // cols, n // cols - 1)
    groups = blocks // 2
    head_dim = kv_weight.shape[1] // 2
    vmem = pl.BlockSpec(memory_space=pltpu.VMEM)
    anywhere = pl.BlockSpec(memory_space=pl.ANY)
    dma = pltpu.SemaphoreType.DMA
    return pl.pallas_call(
        functools.partial(fused, n, cols, reach, head_dim ** (-0.5)),
        out_shape=jax.ShapeDtypeStruct((tok, full), BF16),
        in_specs=[anywhere, anywhere, anywhere, vmem, vmem, vmem, anywhere],
        out_specs=vmem,
        scratch_shapes=[
            pltpu.VMEM((blocks, tok, width), BF16),
            pltpu.VMEM((blocks, width, width), BF16),
            pltpu.VMEM((blocks, width, width), BF16),
            pltpu.VMEM(kv_weight.shape, BF16),
            pltpu.VMEM((tok, tok), BF16),
            pltpu.VMEM((tok, tok), BF16),
            pltpu.VMEM((3, tok, width), F32),
            pltpu.VMEM((3, tok, width), F32),
            pltpu.VMEM((blocks, tok, width), F32),
            pltpu.VMEM((blocks, tok, width), F32),
            pltpu.VMEM((blocks, SUB, width), F32),
            pltpu.VMEM((blocks, SUB, width), F32),
            pltpu.VMEM((groups, 2, 2 * width), F32),
            pltpu.VMEM((n, groups, 2, 2 * width), F32),
            pltpu.VMEM((blocks, 1, width), F32),
            pltpu.VMEM((tok, full), BF16),
            pltpu.VMEM((blocks, tok, width), BF16),
            pltpu.VMEM((n, tok, 2 * head_dim), BF16),
            pltpu.VMEM((blocks, tok, 128), F32),
            pltpu.VMEM((blocks, tok, 128), F32),
            pltpu.VMEM((blocks, tok, width), F32),
            pltpu.VMEM((tok, tok), F32),
            dma((3, blocks)),
            dma,
            dma((n,)),
            dma((n,)),
            dma((levels + 1, PIECES)),
            dma((max(cols - 1, 1), levels + 1, PIECES)),
            dma((n, PIECES)),
        ],
        compiler_params=pltpu.CompilerParams(
            collective_id=0, has_side_effects=True, vmem_limit_bytes=60 * 1024 * 1024
        ),
    )(
        inputs,
        recur_weight,
        input_weight,
        recur_bias.reshape(1, full),
        input_bias.reshape(1, full),
        decay_rate.reshape(1, full),
        kv_weight,
    )


def solution(mesh):
    placed = (P(("batch", "seq"), None), P(), P(), P(), P(), P(), P())
    return jax.shard_map(
        functools.partial(on_device, mesh.shape["seq"]),
        mesh=mesh,
        in_specs=placed,
        out_specs=P(("batch", "seq"), None),
        check_vma=False,
    )
```

profile of v0, /device:TPU:28, one launch (start us, length us, event | category | flops | bytes accessed | tf_op | source)
XLA Modules:
  0.0 71.5 jit_solution(12571326847432853496)
XLA Ops:
  0.0 68.3 %shard_map.73 = bf16[256,4096]{1,0:T(8,128)(2,1)} custom-call(bf16[256,4096]{1,0:T(8,128)(2,1)} %x_hbm.1, bf16[16,256,256]{2,1,0:T(8,128)(2,1)} %rw_hbm.1, bf16[16,256,256]{2,1,0:T(8,128)(2,1)} %iw_hbm.1, f32[1,4096]{1,0:T(1,128)} %bitcast.3, f32[1,4096]{1,0:T(1,128)} %bitcast.4, f32[1,4096]{1,0:T(1,128)} %bitcast.5, bf16[4096,512]{1,0:T(8,128)(2,1)} %kvw_hbm.1), custom_call_target="tpu_custom_call" | custom-call | tf_op jit(solution)/shard_map/pallas_call | solution.py:353
  68.4 3.1 %copy.9 = bf16[256,4096]{1,0:T(8,128)(2,1)} copy(bf16[256,4096]{1,0:T(8,128)(2,1)} %shard_map.73) | data formatting | bytes 4194304
where the time goes:
time: 71.8 us; the launch traced here: 71.5 us
  Pallas kernels  68.3 us (95%)
  local copies, waits for them, and re-layouts  3.13 us (4%)
    pallas_call x1, Pallas kernels, on_device(): pl.pallas_call(functools.partial(fused, n, cols, reach, head_dim ** (-0.5...  68.3 us
    unnamed x1, local copies, waits for them, and re-layouts  3.13 us

commit v1 on v0

--- a/solution.py
+++ b/solution.py
@@ -11,6 +11,8 @@
 WINDOW = 2048
 SUB = 8
 PIECES = 2
+HEADS = 4
+EXTRA = 16
 MESH = pl.DeviceIdType.MESH
 LOG2E = math.log2(math.e)
 F32 = jnp.float32
@@ -30,7 +32,7 @@
     x_hbm, rw_hbm, iw_hbm, rb, ib, dr, kvw_hbm,
     out,
     xv, rwv, iwv, kvw, perm, unperm, pre_a, pre_b, cum, loc, seg_a, seg_s, sum_send, sum_recv,
-    carry, hid, qn, kvb, top, low, acc, bias,
+    carry, hid, qt, kb, vt, top, acc, bias,
     in_sem, kvw_sem, s_send, s_recv, z_send, y_send, kv_recv,
 ):
     me = lax.axis_index("seq")
@@ -40,8 +42,8 @@
     seg = tok // SUB
     groups = blocks // 2
     head_dim = width
+    extra = vt.shape[1] - head_dim
     levels = z_send.shape[0] - 1
-    piece_rows = tok // PIECES
 
     def in_copies(b):
         at = pl.ds(pl.multiple_of(b * width, width), width)
@@ -73,12 +75,19 @@
     place_0 = first // SUB + seg * (first % SUB)
     perm[...] = jnp.where(second == place_0, 1.0, 0.0).astype(BF16)
     unperm[...] = jnp.where(first == place_1, 1.0, 0.0).astype(BF16)
-    bias[...] = jnp.where(place_1 <= first, 0.0, -1e30)
+    bias[...] = jnp.where(place_0 <= place_1, 0.0, -1e30)
+    ones = jnp.where(lax.broadcasted_iota(jnp.int32, (extra, tok), 0) == 0, 1.0, 0.0)
+
+    @pl.loop(0, n)
+    def _(s):
+        vt[s, head_dim:] = ones.astype(BF16)
+
 
     def mats(b, pre):
         for copy in in_copies(b):
             copy.wait()
         moved = dot(perm[...], xv[b])
+        moved = moved * 0.5
         small = moved.astype(BF16)
         pre[0] = moved
         pre[1] = dot(small, rwv[b])
@@ -86,17 +95,18 @@
 
     def gates(b, g, half, pre):
         at = pl.ds(pl.multiple_of(b * width, width), width)
-        rbias = jnp.broadcast_to(rb[:, at], (SUB, width))
-        ibias = jnp.broadcast_to(ib[:, at], (SUB, width))
-        rate = jnp.broadcast_to(dr[:, at] * (-8.0 * LOG2E), (SUB, width))
+        rbias = jnp.broadcast_to(rb[:, at] * 0.5, (SUB, width))
+        ibias = jnp.broadcast_to(ib[:, at] * 0.5, (SUB, width))
+        rate = jnp.broadcast_to(dr[:, at] * (-4.0 * LOG2E), (SUB, width))
         prod = None
         state = None
         for k in range(seg):
             rows = slice(k * SUB, (k + 1) * SUB)
-            rec = 0.5 * jnp.tanh(0.5 * (pre[1, rows, :] + rbias)) + 0.5
-            gate = 0.5 * jnp.tanh(0.5 * (pre[2, rows, :] + ibias)) + 0.5
-            step = jnp.exp2(rec * rate)
-            drive = jnp.sqrt(1.0 - step * step) * (gate * pre[0, rows, :])
+            rec = jnp.tanh(pre[1, rows, :] + rbias)
+            gate = jnp.tanh(pre[2, rows, :] + ibias) + 1.0
+            step = jnp.exp2(rec * rate + rate)
+            rest = jnp.maximum(1.0 - step * step, 1e-36)
+            drive = (rest * lax.rsqrt(rest)) * (gate * pre[0, rows, :])
             prod = step if k == 0 else prod * step
             state = drive if k == 0 else step * state + drive
             cum[b, rows, :] = prod
@@ -173,14 +183,14 @@
             twice = jnp.concatenate([into, into], axis=0)
             hid[rows, at] = (loc[b, rows, :] + cum[b, rows, :] * twice).astype(BF16)
 
-    kvw_copy.wait()
-    kvb[me] = dot(hid[...], kvw[...]).astype(BF16)
+    def piece_of(s, piece):
+        return kb.at[s] if piece == 0 else vt.at[s, pl.ds(0, head_dim)]
 
     def z_copy(s, m, piece):
-        rows = pl.ds(piece * piece_rows, piece_rows)
+        part = piece_of(s, piece)
         return pltpu.make_async_remote_copy(
-            src_ref=kvb.at[s, rows],
-            dst_ref=kvb.at[s, rows],
+            src_ref=part,
+            dst_ref=part,
             send_sem=z_send.at[m, piece],
             recv_sem=kv_recv.at[s, piece],
             device_id={"seq": me + cols},
@@ -188,11 +198,11 @@
         )
 
     def y_copy(s, m, piece, delta):
-        rows = pl.ds(piece * piece_rows, piece_rows)
+        part = piece_of(s, piece)
         to = row * cols + lax.rem(col + delta, cols)
         return pltpu.make_async_remote_copy(
-            src_ref=kvb.at[s, rows],
-            dst_ref=kvb.at[s, rows],
+            src_ref=part,
+            dst_ref=part,
             send_sem=y_send.at[delta - 1, m, piece],
             recv_sem=kv_recv.at[s, piece],
             device_id={"seq": to},
@@ -200,10 +210,10 @@
         )
 
     def arrived(s, piece):
-        rows = pl.ds(piece * piece_rows, piece_rows)
+        part = piece_of(s, piece)
         pltpu.make_async_remote_copy(
-            src_ref=kvb.at[s, rows],
-            dst_ref=kvb.at[s, rows],
+            src_ref=part,
+            dst_ref=part,
             send_sem=z_send.at[0, piece],
             recv_sem=kv_recv.at[s, piece],
             device_id={"seq": lax.rem(me + cols, n)},
@@ -227,51 +237,43 @@
             def _():
                 y_copy(s, m, piece, delta).start()
 
-    for piece in range(PIECES):
-        forward(me, 0, piece)
+    kvw_copy.wait()
+    kb[me] = dot(hid[...], kvw[:, :head_dim]).astype(BF16)
+    forward(me, 0, 0)
+    vt[me, :head_dim] = dot(hid[...], kvw[:, head_dim:]).T.astype(BF16)
+    forward(me, 0, 1)
 
     factor = scale * LOG2E
 
-    @pl.loop(0, blocks, step=2)
+    @pl.loop(0, blocks, step=HEADS)
     def _(base):
-        for h in (base, base + 1):
+        for h in [base + i for i in range(HEADS)]:
             at = pl.ds(pl.multiple_of(h * width, width), width)
-            query = dot(unperm[...], hid[:, at]).astype(BF16)
-            qn[h] = query
-            scores = dot_t(query, kvb[me, :, :head_dim]) + bias[...]
-            highest = jnp.max(scores, axis=1, keepdims=True)
-            expo = jnp.exp2((scores - highest) * factor)
-            top[h] = jnp.broadcast_to(highest, (tok, 128))
-            low[h] = functools.reduce(
-                jnp.add, [expo[:, c : c + 128] for c in range(0, tok, 128)]
-            )
-            acc[h] = dot(expo.astype(BF16), kvb[me, :, head_dim:])
+            query = hid[:, at].astype(F32).T.astype(BF16)
+            qt[h] = query
+            scores = dot(kb[me], query) + bias[...]
+            highest = jnp.max(scores, axis=0, keepdims=True)
+            top[h] = highest
+            expo = jnp.exp2((scores - highest) * factor).astype(BF16)
+            acc[h] = dot(vt[me], expo)
 
     def attend(s, far, masked):
-        @pl.loop(0, blocks, step=2)
+        @pl.loop(0, blocks, step=HEADS)
         def _(base):
-            for h in (base, base + 1):
-                scores = dot_t(qn[h], kvb[s, :, :head_dim])
+            for h in [base + i for i in range(HEADS)]:
+                scores = dot(kb[s], qt[h])
                 if masked:
-                    qrow = lax.broadcasted_iota(jnp.int32, (tok, tok), 0)
-                    krow = lax.broadcasted_iota(jnp.int32, (tok, tok), 1)
+                    krow = lax.broadcasted_iota(jnp.int32, (tok, tok), 0)
                     krow = krow // SUB + seg * (krow % SUB)
+                    qrow = lax.broadcasted_iota(jnp.int32, (tok, tok), 1)
+                    qrow = qrow // SUB + seg * (qrow % SUB)
                     scores = jnp.where(far * tok + qrow - krow < WINDOW, scores, -1e30)
                 before = top[h]
-                highest = jnp.maximum(before, jnp.max(scores, axis=1, keepdims=True))
+                highest = jnp.maximum(before, jnp.max(scores, axis=0, keepdims=True))
                 shrink = jnp.exp2((before - highest) * factor)
-                parts = [
-                    jnp.exp2((scores[:, c : c + 128] - highest) * factor)
-                    for c in range(0, tok, 128)
-                ]
                 top[h] = highest
-                low[h] = low[h] * shrink + functools.reduce(jnp.add, parts)
-                expo = jnp.concatenate([p.astype(BF16) for p in parts], axis=1)
-                update = dot(expo, kvb[s, :, head_dim:])
-                for c in range(0, head_dim, 128):
-                    acc[h, :, c : c + 128] = (
-                        acc[h, :, c : c + 128] * shrink + update[:, c : c + 128]
-                    )
+                expo = jnp.exp2((scores - highest) * factor).astype(BF16)
+                acc[h] = acc[h] * shrink + dot(vt[s], expo)
 
     partial = reach * tok + tok - 1 >= WINDOW
 
@@ -315,8 +317,8 @@
     @pl.loop(0, blocks)
     def _(h):
         at = pl.ds(pl.multiple_of(h * width, width), width)
-        total = jnp.sum(low[h], axis=1, keepdims=True)
-        out[:, at] = (acc[h] * (1.0 / total)).astype(BF16)
+        mean = acc[h, :head_dim] * (1.0 / acc[h, head_dim : head_dim + 1])
+        out[:, at] = dot_t(unperm[...], mean.astype(BF16)).astype(BF16)
 
     @pl.loop(me + 1, n)
     def _(to):
@@ -372,11 +374,11 @@
             pltpu.VMEM((n, groups, 2, 2 * width), F32),
             pltpu.VMEM((blocks, 1, width), F32),
             pltpu.VMEM((tok, full), BF16),
-            pltpu.VMEM((blocks, tok, width), BF16),
-            pltpu.VMEM((n, tok, 2 * head_dim), BF16),
-            pltpu.VMEM((blocks, tok, 128), F32),
-            pltpu.VMEM((blocks, tok, 128), F32),
-            pltpu.VMEM((blocks, tok, width), F32),
+            pltpu.VMEM((blocks, head_dim, tok), BF16),
+            pltpu.VMEM((n, tok, head_dim), BF16),
+            pltpu.VMEM((n, head_dim + EXTRA, tok), BF16),
+            pltpu.VMEM((blocks, 1, tok), F32),
+            pltpu.VMEM((blocks, head_dim + EXTRA, tok), F32),
             pltpu.VMEM((tok, tok), F32),
             dma((3, blocks)),
             dma,

time: 71.8 us -> 52.1 us (0.73)
  Pallas kernels: 68.3 us -> 48.3 us
    pallas_call x1, Pallas kernels: 68.3 us -> 48.3 us  [on_device(): pl.pallas_call(functools.partial(fused, n, cols, reach, head_dim ** (-0.5...]
where the time goes in v1:
time: 52.1 us; the launch traced here: 51.5 us
  Pallas kernels  48.3 us (93%)
  local copies, waits for them, and re-layouts  3.13 us (6%)
    pallas_call x1, Pallas kernels, on_device(): pl.pallas_call(functools.partial(fused, n, cols, reach, head_dim ** (-0.5...  48.3 us
    unnamed x1, local copies, waits for them, and re-layouts  3.13 us

profile of v1, /device:TPU:28, one launch (start us, length us, event | category | flops | bytes accessed | tf_op | source)
XLA Modules:
  0.0 51.5 jit_solution(1690371934167698987)
XLA Ops:
  0.0 48.3 %shard_map.73 = bf16[256,4096]{1,0:T(8,128)(2,1)} custom-call(bf16[256,4096]{1,0:T(8,128)(2,1)} %x_hbm.1, bf16[16,256,256]{2,1,0:T(8,128)(2,1)} %rw_hbm.1, bf16[16,256,256]{2,1,0:T(8,128)(2,1)} %iw_hbm.1, f32[1,4096]{1,0:T(1,128)} %bitcast.3, f32[1,4096]{1,0:T(1,128)} %bitcast.4, f32[1,4096]{1,0:T(1,128)} %bitcast.5, bf16[4096,512]{1,0:T(8,128)(2,1)} %kvw_hbm.1), custom_call_target="tpu_custom_call" | custom-call | tf_op jit(solution)/shard_map/pallas_call | solution.py:355
  48.4 3.1 %copy.9 = bf16[256,4096]{1,0:T(8,128)(2,1)} copy(bf16[256,4096]{1,0:T(8,128)(2,1)} %shard_map.73) | data formatting | bytes 4194304

commit v2 on v1

--- a/solution.py
+++ b/solution.py
@@ -11,7 +11,7 @@
 WINDOW = 2048
 SUB = 8
 PIECES = 2
-HEADS = 4
+HEADS = 16
 EXTRA = 16
 MESH = pl.DeviceIdType.MESH
 LOG2E = math.log2(math.e)
@@ -174,14 +174,15 @@
         carry[2 * g] = entering[g][:, :width]
         carry[2 * g + 1] = entering[g][:, width:]
 
-    @pl.loop(0, blocks)
-    def _(b):
-        at = pl.ds(pl.multiple_of(b * width, width), width)
-        into = seg_s[b] + seg_a[b] * carry[b]
-        for k in range(seg // 2):
-            rows = slice(2 * k * SUB, (2 * k + 2) * SUB)
+    @pl.loop(0, blocks, step=2)
+    def _(base):
+        for b in (base, base + 1):
+            at = pl.ds(pl.multiple_of(b * width, width), width)
+            into = seg_s[b] + seg_a[b] * carry[b]
             twice = jnp.concatenate([into, into], axis=0)
-            hid[rows, at] = (loc[b, rows, :] + cum[b, rows, :] * twice).astype(BF16)
+            for k in range(seg // 2):
+                rows = slice(2 * k * SUB, (2 * k + 2) * SUB)
+                hid[rows, at] = (loc[b, rows, :] + cum[b, rows, :] * twice).astype(BF16)
 
     def piece_of(s, piece):
         return kb.at[s] if piece == 0 else vt.at[s, pl.ds(0, head_dim)]
@@ -314,11 +315,12 @@
                 def _():
                     attend(s, far, False)
 
-    @pl.loop(0, blocks)
-    def _(h):
-        at = pl.ds(pl.multiple_of(h * width, width), width)
-        mean = acc[h, :head_dim] * (1.0 / acc[h, head_dim : head_dim + 1])
-        out[:, at] = dot_t(unperm[...], mean.astype(BF16)).astype(BF16)
+    @pl.loop(0, blocks, step=HEADS)
+    def _(base):
+        for h in [base + i for i in range(HEADS)]:
+            at = pl.ds(pl.multiple_of(h * width, width), width)
+            mean = acc[h, :head_dim] * (1.0 / acc[h, head_dim : head_dim + 1])
+            out[:, at] = dot_t(unperm[...], mean.astype(BF16)).astype(BF16)
 
     @pl.loop(me + 1, n)
     def _(to):

time: 52.1 us -> 46.6 us (0.89)
  Pallas kernels: 48.3 us -> 43 us
    pallas_call x1, Pallas kernels: 48.3 us -> 43 us  [on_device(): pl.pallas_call(functools.partial(fused, n, cols, reach, head_dim ** (-0.5...]
where the time goes in v2:
time: 46.6 us; the launch traced here: 46.2 us
  Pallas kernels  43 us (92%)
  local copies, waits for them, and re-layouts  3.13 us (7%)
    pallas_call x1, Pallas kernels, on_device(): pl.pallas_call(functools.partial(fused, n, cols, reach, head_dim ** (-0.5...  43 us
    unnamed x1, local copies, waits for them, and re-layouts  3.13 us

profile of v2, /device:TPU:28, one launch (start us, length us, event | category | flops | bytes accessed | tf_op | source)
XLA Modules:
  0.0 46.2 jit_solution(13920134796355356036)
XLA Ops:
  0.0 43.0 %shard_map.73 = bf16[256,4096]{1,0:T(8,128)(2,1)} custom-call(bf16[256,4096]{1,0:T(8,128)(2,1)} %x_hbm.1, bf16[16,256,256]{2,1,0:T(8,128)(2,1)} %rw_hbm.1, bf16[16,256,256]{2,1,0:T(8,128)(2,1)} %iw_hbm.1, f32[1,4096]{1,0:T(1,128)} %bitcast.3, f32[1,4096]{1,0:T(1,128)} %bitcast.4, f32[1,4096]{1,0:T(1,128)} %bitcast.5, bf16[4096,512]{1,0:T(8,128)(2,1)} %kvw_hbm.1), custom_call_target="tpu_custom_call" | custom-call | tf_op jit(solution)/shard_map/pallas_call | solution.py:357
  43.0 3.1 %copy.9 = bf16[256,4096]{1,0:T(8,128)(2,1)} copy(bf16[256,4096]{1,0:T(8,128)(2,1)} %shard_map.73) | data formatting | bytes 4194304
